TPU v7x, 32 devices: a whole 2x2x4 slice. The times are simulated.
32 devices in a mesh: gx: 2 (over x), gy: 4 (over y, core), gz: 4 (over z).
Axes of the slice: x: 2, y: 2, z: 4, core: 2. Of those that a mesh axis runs over, the one named last changes fastest.
Arguments:
- query: bfloat16 [4, 4, 4096], replicated, may hold values from -50 to 50
- keys: bfloat16 [4096, 4, 4096], P(('gx', 'gy', 'gz')), may hold values from -6 to 6
- values: bfloat16 [4096, 4, 4096], P(('gx', 'gy', 'gz')), may hold values from -6 to 6
- lm_keys: bfloat16 [128, 4, 4096], P(('gx', 'gy', 'gz')), may hold values from -10 to 10
- lm_values: bfloat16 [128, 4, 4096], P(('gx', 'gy', 'gz')), may hold values from -6 to 6
- selected: int32 [4, 16, 16], replicated, may hold values from 0 to 127, as said below
Outputs:
- attended: float32 [4, 4, 4096], P(None, None, ('gx', 'gy', 'gz'))
Inputs may be any that keep to these rules, and one draw needn't show every extreme that they name: `selected`: each batch row and head names 16 different blocks; every shard holds either none of them or exactly 2.
All inputs are finite; a program needn't handle non-finite values.
Results may differ from a plain program's by a relative error of at most 0.0007.
Values sent between devices are 32-bit elements; how exact they have to be, the bound alone decides.
A program may use at most 64 MiB of HBM per device.

v0:
```python
import math

import jax
import jax.numpy as jnp
from jax import lax
from jax.sharding import PartitionSpec as P


def body(query, keys, values, lm_keys, lm_values, selected):
    device_count = lax.axis_size(("gx", "gy", "gz"))
    my_index = lax.axis_index(("gx", "gy", "gz"))
    positions, batch_rows, feature_width = keys.shape
    local_blocks = lm_keys.shape[0]
    block_len = positions // local_blocks
    head_count = selected.shape[1]
    head_width = feature_width // head_count
    draft_count = query.shape[1]
    query_heads = query.reshape(batch_rows, draft_count, head_count, head_width)
    score_scale = 1.0 / math.sqrt(head_width)
    block_ids = my_index * local_blocks + jnp.arange(local_blocks, dtype=jnp.int32)
    chosen_here = jnp.any(selected[:, :, :, None] == block_ids[None, None, None, :], axis=2)
    summary_keys = lm_keys.reshape(local_blocks, batch_rows, head_count, head_width)
    summary_values = lm_values.reshape(local_blocks, batch_rows, head_count, head_width)
    summary_score = (
        jnp.einsum("bphd,lbhd->bphl", query_heads, summary_keys, preferred_element_type=jnp.float32)
        * score_scale
    )
    keys_heads = keys.reshape(positions, batch_rows, head_count, head_width)
    values_heads = values.reshape(positions, batch_rows, head_count, head_width)
    live_tokens = jnp.repeat(chosen_here, block_len, axis=2)
    token_score = (
        jnp.einsum("bphd,tbhd->bpht", query_heads, keys_heads, preferred_element_type=jnp.float32)
        * score_scale
    )
    token_score = jnp.where(live_tokens[:, None], token_score, -jnp.inf)
    local_peak = jnp.maximum(jnp.max(token_score, -1), jnp.max(summary_score, -1))
    token_weight = jnp.exp(token_score - local_peak[..., None])
    summary_weight = jnp.exp(summary_score - local_peak[..., None])
    local_total = jnp.sum(token_weight, -1) + jnp.sum(summary_weight, -1)
    local_sum = jnp.einsum(
        "bpht,tbhd->bphd",
        token_weight.astype(jnp.bfloat16),
        values_heads,
        preferred_element_type=jnp.float32,
    ) + jnp.einsum(
        "bphl,lbhd->bphd",
        summary_weight.astype(jnp.bfloat16),
        summary_values,
        preferred_element_type=jnp.float32,
    )
    column_count = feature_width // device_count
    global_peak = lax.pmax(local_peak, ("gx", "gy", "gz"))
    rescale = jnp.exp(local_peak - global_peak)
    denominator, numerator = lax.psum(
        (local_total * rescale, local_sum * rescale[..., None]), ("gx", "gy", "gz")
    )
    own_numerator = lax.dynamic_slice_in_dim(
        numerator.reshape(batch_rows, draft_count, feature_width),
        my_index * column_count,
        column_count,
        2,
    )
    spread_denominator = jnp.repeat(denominator, head_width, axis=2)
    own_denominator = lax.dynamic_slice_in_dim(
        spread_denominator, my_index * column_count, column_count, 2
    )
    return own_numerator / own_denominator


def solution(mesh):
    placed = (
        P(),
        P(("gx", "gy", "gz"), None, None),
        P(("gx", "gy", "gz"), None, None),
        P(("gx", "gy", "gz"), None, None),
        P(("gx", "gy", "gz"), None, None),
        P(),
    )
    return jax.shard_map(
        body,
        mesh=mesh,
        in_specs=placed,
        out_specs=P(None, None, ("gx", "gy", "gz")),
        check_vma=False,
    )
```

profile of v0, /device:TPU:0, one launch (start us, length us, event | category | flops | bytes accessed | tf_op | source)
XLA Modules:
  0.0 211.6 jit_solution(752959228649032096)
XLA Ops:
  6.5 0.0 copy-start
  6.5 0.0 all-reduce.2.cloned.1.call-start
  6.5 1.2 compare_reduce_fusion
  7.8 0.1 copy.15
  7.9 0.1 broadcast_in_dim.25
  8.0 0.1 broadcast_in_dim.26
  8.1 0.0 copy-start.1
  8.2 7.7 %reshape.33 = bf16[128,4,16,256]{3,2,1,0:T(8,128)(2,1)} reshape(bf16[128,4,4096]{2,1,0:T(4,128)(2,1)} %param.7) | data formatting | bytes 8388608 | tf_op jit(solution)/shard_map/reshape | solution.py:28
  15.9 0.0 copy-done.1
  15.9 0.1 reshape.35
  16.0 0.0 copy-done
  16.0 0.2 fusion.27
  16.2 4.6 %fusion.26 = (f32[4,4,16]{1,2,0:T(8,128)S(1)}, f32[4,4,16,128]{3,1,2,0:T(4,128)S(1)}) fusion(bf16[4,4,16,256]{3,1,2,0:T(4,128)(2,1)S(1)} %bitcast.15, bf16[128,4,16,256]{3,2,1,0:T(8,128)(2,1)} %reshape.33, pred[4,16,128]{2,1,0:T(8,128)(4,1)S(1)} %broadcast_in_dim.26), kind=kOutput, calls=%fused_computation.27 | convolution fusion | flops 16875264 | bytes 4465664 | tf_op jit(solution)/shard_map/bphd,tbhd->bpht/dot_general | solution.py:32
  20.9 42.1 %pmax.7 = f32[4,4,16]{1,2,0:T(8,128)S(1)} all-reduce(f32[4,4,16]{1,2,0:T(8,128)S(1)} %max.9), channel_id=1, replica_groups=mesh['gx'=2,'gy'=4,'gz'=4] {'gx','gy','gz'}, use_global_device_ids=true, to_apply=%region_3.4 | all-reduce | flops 256 | bytes 2048 | tf_op jit(solution)/shard_map/pmax | solution.py:52
  63.0 0.3 fusion.18
  63.2 0.1 fusion.20
  63.4 7.7 %reshape.36 = bf16[128,4,16,256]{3,2,1,0:T(8,128)(2,1)} reshape(bf16[128,4,4096]{2,1,0:T(4,128)(2,1)} %param.8) | data formatting | bytes 8388608 | tf_op jit(solution)/shard_map/reshape | solution.py:29
  71.1 0.0 copy-start.2
  71.1 4.6 %fusion = f32[4,16,4,256]{3,2,1,0:T(4,128)S(1)} fusion(bf16[128,4,16,256]{3,2,1,0:T(8,128)(2,1)} %reshape.36, f32[4,4,16,128]{3,1,2,0:T(4,128)S(1)} %get-tuple-element.8, f32[4,4,16]{1,2,0:T(8,128)S(1)} %max.9), kind=kOutput, calls=%fused_computation | convolution fusion | flops 16842752 | bytes 4588544 | tf_op jit(solution)/shard_map/bpht,tbhd->bphd/dot_general | solution.py:40
  75.7 0.0 copy-done.2
  75.7 0.1 reshape.37
  75.8 1.0 fusion.5
  76.7 0.0 all-reduce.2.cloned.1.call-update
  76.8 40.3 %psum.15 = f32[4,4,16]{1,2,0:T(8,128)S(1)} all-reduce(f32[4,4,16]{1,2,0:T(8,128)S(1)} %get-tuple-element.5), channel_id=1, replica_groups=mesh['gx'=2,'gy'=4,'gz'=4] {'gx','gy','gz'}, use_global_device_ids=true, to_apply=%region_7.8 | all-reduce | flops 256 | bytes 2048 | tf_op jit(solution)/shard_map/psum | solution.py:54
  117.1 0.1 copy.23
  117.2 0.1 broadcast_in_dim.29
  117.3 0.1 reshape.39
  117.4 86.0 %all-reduce.2.cloned.1.call-done = f32[4,4,4096]{2,1,0:T(4,128)} async-done(((f32[4,4,4096]{2,1,0:T(4,128)}), f32[4,4,4096]{2,1,0:T(4,128)}) %all-reduce.2.cloned.1.call-update) | async-done | bytes 262160 | tf_op jit(solution)/shard_map/psum | solution.py:54
  203.4 1.3 dynamic-slice_divide_fusion
  (3 shorter events, 0.0 us)
Async XLA Ops:
  6.5 9.4 %copy-start = (bf16[4,4,4096]{2,1,0:T(4,128)(2,1)S(1)}, bf16[4,4,4096]{2,1,0:T(4,128)(2,1)}, u32[]{:S(2)}) copy-start(bf16[4,4,4096]{2,1,0:T(4,128)(2,1)} %param.6) | copy-start | bytes 393220
  6.5 196.9 %all-reduce.2.cloned.1.call-start = ((), (), s32[]{:S(2)}) async-start(), calls=%async_computation | async-start | bytes 524288 | tf_op jit(solution)/shard_map/psum | solution.py:54
  8.1 7.8 %copy-start.1 = (bf16[4,4,4096]{2,1,0:T(4,128)(2,1)S(1)}, bf16[4,4,4096]{2,1,0:T(4,128)(2,1)}, u32[]{:S(2)}) copy-start(bf16[4,4,4096]{2,1,0:T(4,128)(2,1)} %param.9) | copy-start | bytes 393220
  71.1 4.6 %copy-start.2 = (bf16[4,4,4096]{2,1,0:T(4,128)(2,1)S(1)}, bf16[4,4,4096]{2,1,0:T(4,128)(2,1)}, u32[]{:S(2)}) copy-start(bf16[4,4,4096]{2,1,0:T(4,128)(2,1)} %param.10) | copy-start | bytes 393220
Sparse Core Ops, SparseCore 0:
  76.9 126.4 all-reduce.1
where the time goes:
time: 212 us
  waiting for transfers between devices  86 us (41%)
  blocking collectives  82.4 us (39%)
  local copies, waits for them, and re-layouts  16.3 us (8%)
  between operations  13.5 us (6%)
  matrix products  10.4 us (5%)
  other arithmetic  2.92 us (1%)
    psum x1, waiting for transfers between devices, body(): lax.psum((local_total * rescale, local_sum * rescale[..., None]), ('gx',...  86 us
    pmax x1, blocking collectives, body(): global_peak = lax.pmax(local_peak, ('gx', 'gy', 'gz'))  42.1 us
    psum x1, blocking collectives, body(): lax.psum((local_total * rescale, local_sum * rescale[..., None]), ('gx',...  40.3 us
    reshape x1, local copies, waits for them, and re-layouts, body(): keys_heads = keys.reshape(positions, batch_rows, head_count, head_width)  7.75 us
    reshape x1, local copies, waits for them, and re-layouts, body(): values_heads = values.reshape(positions, batch_rows, head_count, head_width)  7.71 us
    dot_general x1, matrix products, body(): jnp.einsum('bphd,tbhd->bpht', query_heads, keys_heads, preferred_element_...  4.65 us
    dot_general x1, matrix products, body(): jnp.einsum('bpht,tbhd->bphd', token_weight.astype(jnp.bfloat16), values_h...  4.58 us
  transfers between devices with their start and end apart: 1, of which 1 were waited for; matrix products, arithmetic and copies ran while one was open for 0% of the time, Pallas kernels for 0%

commit v1 on v0

v1 whole, which is shorter than its diff:
```python
import functools
import math

import jax
import jax.numpy as jnp
from jax import lax
from jax.experimental import pallas as pl
from jax.experimental.pallas import tpu as pltpu
from jax.sharding import PartitionSpec as P

AXES = ("gx", "gy", "gz")
LANES = 128
GROUPS = 4
NEG = float("-inf")


def kernel(sizes, cfg, q_hbm, k_hbm, v_hbm, lk_hbm, lv_hbm, sel_ref, out_ref,
           qbuf, kbuf, vbuf, send, recv, qsem, ksem, vsem, send_sem, recv_sem):
    positions, batch, local_blocks, heads, width, drafts, columns = cfg
    nx, ny, nz = sizes
    count = nx * ny * nz
    me = (lax.axis_index("gx") * ny + lax.axis_index("gy")) * nz + lax.axis_index("gz")
    per_head = width // LANES
    tiles = heads * per_head
    sharers = LANES // columns
    rows = batch * drafts
    tokens = positions * batch
    group_heads = heads // GROUPS
    group_tiles = group_heads * per_head
    my_group = (me // sharers) // group_tiles
    scale = 1.0 / math.sqrt(width)

    def device_of(d):
        return {"gx": d // (ny * nz), "gy": (d // nz) % ny, "gz": d % nz}

    def group_at(step):
        return lax.rem(my_group + 1 + step, GROUPS)

    for step in range(GROUPS):
        g = group_at(step)

        def start(i, _, g=g, step=step):
            c = g * group_tiles + i
            cols = pl.ds(pl.multiple_of(c * LANES, LANES), LANES)
            pltpu.make_async_copy(q_hbm.at[:, :, cols], qbuf.at[c], qsem.at[step]).start()
            pltpu.make_async_copy(lk_hbm.at[:, :, cols], kbuf.at[c, pl.ds(positions, local_blocks)], ksem.at[step]).start()
            pltpu.make_async_copy(k_hbm.at[:, :, cols], kbuf.at[c, pl.ds(0, positions)], ksem.at[step]).start()
            pltpu.make_async_copy(lv_hbm.at[:, :, cols], vbuf.at[c, pl.ds(positions, local_blocks)], vsem.at[step]).start()
            pltpu.make_async_copy(v_hbm.at[:, :, cols], vbuf.at[c, pl.ds(0, positions)], vsem.at[step]).start()
            return 0

        lax.fori_loop(0, group_tiles, start, 0)

    barrier = pltpu.get_barrier_semaphore()

    def greet(i, _):
        pl.semaphore_signal(barrier, inc=1, device_id=device_of(lax.rem(me + i, count)), device_id_type=pl.DeviceIdType.MESH)
        return 0

    lax.fori_loop(1, count, greet, 0)

    total_rows = tokens + local_blocks * batch
    block_cols = tokens // local_blocks
    same = (lax.broadcasted_iota(jnp.int32, (rows, block_cols), 1) % batch
            == lax.broadcasted_iota(jnp.int32, (rows, block_cols), 0) // drafts)
    same_lm = same[:, :local_blocks * batch]
    lm_bias = jnp.where(same_lm, 0.0, NEG)
    lane = lax.broadcasted_iota(jnp.int32, (rows, LANES), 1)
    row = lax.broadcasted_iota(jnp.int32, (rows, LANES), 0)

    def compute(step, _):
        g = group_at(step)
        span = pl.ds(g * group_tiles, group_tiles)
        pltpu.make_async_copy(qbuf.at[span], qbuf.at[span], qsem.at[step]).wait()
        pltpu.make_async_copy(kbuf.at[span], kbuf.at[span], ksem.at[step]).wait()
        probs = []
        stats = []
        for i in range(group_heads):
            h = g * group_heads + i
            q = jnp.concatenate([qbuf[h * per_head + c].reshape(rows, LANES) for c in range(per_head)], axis=1)
            k = jnp.concatenate([kbuf[h * per_head + c].reshape(total_rows, LANES) for c in range(per_head)], axis=1)
            s = lax.dot_general(q, k, (((1,), (1,)), ((), ())), preferred_element_type=jnp.float32) * scale
            chosen = jnp.concatenate(
                [jnp.broadcast_to(sel_ref[b, pl.ds(h, 1), :], (drafts, sel_ref.shape[2])) for b in range(batch)], axis=0)
            parts = []
            for j in range(local_blocks):
                hit = jnp.max(jnp.where(chosen == me * local_blocks + j, 1, 0), axis=1, keepdims=True)
                parts.append(jnp.where(same & (hit > 0), 0.0, NEG))
            s = s + jnp.concatenate(parts + [lm_bias], axis=1)
            peak = jnp.max(s, axis=1, keepdims=True)
            w = jnp.exp(s - peak)
            total = jnp.sum(w, axis=1, keepdims=True)
            probs.append(w.astype(jnp.bfloat16))
            spread = jnp.where(lane == row, peak, jnp.where(lane == row + rows, total, 0.0))
            stats.append(jnp.sum(spread, axis=0, keepdims=True))
        pltpu.make_async_copy(vbuf.at[span], vbuf.at[span], vsem.at[step]).wait()
        for i in range(group_heads):
            h = g * group_heads + i
            v = jnp.concatenate([vbuf[h * per_head + c].reshape(total_rows, LANES) for c in range(per_head)], axis=1)
            o = jnp.dot(probs[i], v, preferred_element_type=jnp.float32)
            for c in range(per_head):
                u = h * per_head + c
                send[u, pl.ds(0, rows), :] = o[:, c * LANES:(c + 1) * LANES]
                send[u, pl.ds(rows, 8), :] = jnp.broadcast_to(stats[i], (8, LANES))

        @pl.when(step == 0)
        def _():
            pl.semaphore_wait(barrier, count - 1)

        def post(i, _):
            d = g * group_tiles * sharers + i
            u = d // sharers

            @pl.when(d == me)
            def _():
                pltpu.make_async_copy(send.at[u], recv.at[me], recv_sem).start()

            @pl.when(d != me)
            def _():
                pltpu.make_async_remote_copy(
                    src_ref=send.at[u], dst_ref=recv.at[me], send_sem=send_sem, recv_sem=recv_sem,
                    device_id=device_of(d), device_id_type=pl.DeviceIdType.MESH).start()
            return 0

        lax.fori_loop(0, group_tiles * sharers, post, 0)
        return 0

    lax.fori_loop(0, GROUPS, compute, 0)

    pltpu.make_async_copy(recv, recv, recv_sem).wait()
    gathered = recv[:, rows, :]
    flipped = gathered.T
    peaks = flipped[:rows]
    totals = flipped[rows:2 * rows]
    top = jnp.max(peaks, axis=1, keepdims=True)
    factor = jnp.exp(peaks - top)
    denominator = jnp.sum(factor * totals, axis=1, keepdims=True)
    numerator = jnp.zeros((rows, LANES), jnp.float32)
    for s in range(count):
        numerator = numerator + factor[:, s:s + 1] * recv[s, pl.ds(0, rows), :]
    out_ref[...] = (numerator / denominator).reshape(batch, drafts, LANES)
    others = pl.ds(0, count - 1)
    pltpu.make_async_copy(recv.at[others], recv.at[others], send_sem).wait()


def body(sizes, query, keys, values, lm_keys, lm_values, selected):
    positions, batch, feature = keys.shape
    local_blocks = lm_keys.shape[0]
    heads = selected.shape[1]
    width = feature // heads
    drafts = query.shape[1]
    count = math.prod(sizes)
    columns = feature // count
    tiles = feature // LANES
    rows = batch * drafts
    cfg = (positions, batch, local_blocks, heads, width, drafts, columns)
    anywhere = pl.BlockSpec(memory_space=pl.ANY)
    vmem = pl.BlockSpec(memory_space=pltpu.VMEM)
    span = positions + local_blocks
    out = pl.pallas_call(
        functools.partial(kernel, sizes, cfg),
        out_shape=jax.ShapeDtypeStruct((batch, drafts, LANES), jnp.float32),
        in_specs=[anywhere] * 5 + [vmem],
        out_specs=vmem,
        scratch_shapes=[
            pltpu.VMEM((tiles, batch, drafts, LANES), jnp.bfloat16),
            pltpu.VMEM((tiles, span, batch, LANES), jnp.bfloat16),
            pltpu.VMEM((tiles, span, batch, LANES), jnp.bfloat16),
            pltpu.VMEM((tiles, rows + 8, LANES), jnp.float32),
            pltpu.VMEM((count, rows + 8, LANES), jnp.float32),
            pltpu.SemaphoreType.DMA((GROUPS,)),
            pltpu.SemaphoreType.DMA((GROUPS,)),
            pltpu.SemaphoreType.DMA((GROUPS,)),
            pltpu.SemaphoreType.DMA,
            pltpu.SemaphoreType.DMA,
        ],
        compiler_params=pltpu.CompilerParams(collective_id=0, has_side_effects=True),
        name="block_attention",
    )(query, keys, values, lm_keys, lm_values, selected)
    if columns < LANES:
        me = lax.axis_index(AXES)
        out = lax.dynamic_slice_in_dim(out, (me * columns) % LANES, columns, 2)
    return out


def solution(mesh):
    sizes = tuple(mesh.shape[a] for a in AXES)
    split = P(AXES, None, None)
    return jax.shard_map(
        functools.partial(body, sizes),
        mesh=mesh,
        in_specs=(P(), split, split, split, split, P()),
        out_specs=P(None, None, AXES),
        check_vma=False,
    )
```

time: 212 us -> 20.5 us (0.10)
  waiting for transfers between devices: 86 us -> 0 us
  blocking collectives: 82.4 us -> 0 us
  Pallas kernels: 0 us -> 18.9 us
  local copies, waits for them, and re-layouts: 16.3 us -> 1.3 us
  between operations: 13.5 us -> 0.01 us
  matrix products: 10.4 us -> 0 us
  other arithmetic: 2.92 us -> 0 us
    psum x1 -> x0, waiting for transfers between devices: 86 us -> none  [body(): lax.psum((local_total * rescale, local_sum * rescale[..., None]), ('gx',...]
    pmax x1 -> x0, blocking collectives: 42.1 us -> none  [body(): global_peak = lax.pmax(local_peak, ('gx', 'gy', 'gz'))]
    psum x1 -> x0, blocking collectives: 40.3 us -> none  [body(): lax.psum((local_total * rescale, local_sum * rescale[..., None]), ('gx',...]
    pallas_call x0 -> x1, Pallas kernels: none -> 18.9 us  [body(): pl.pallas_call(functools.partial(kernel, sizes, cfg), out_shape=jax.Shape...]
    reshape x5 -> x0, local copies, waits for them, and re-layouts: 15.7 us -> none  [the longest x1 7.75 us: body(): keys_heads = keys.reshape(positions, batch_rows, head_count, head_width)]
    dot_general x4 -> x0, matrix products: 10.4 us -> none  [the longest x1 4.65 us: body(): jnp.einsum('bphd,tbhd->bpht', query_heads, keys_heads, preferred_element_...]
  transfers between devices with their start and end apart: 1 -> 0, of which waited for: 1 -> 0; matrix products, arithmetic and copies ran while one was open for 0% -> 0% of each run, Pallas kernels for 0% -> 0%
where the time goes in v1:
time: 20.5 us; the launch traced here: 20.2 us
  Pallas kernels  18.9 us (92%)
  local copies, waits for them, and re-layouts  1.3 us (6%)
    pallas_call x1, Pallas kernels, body(): pl.pallas_call(functools.partial(kernel, sizes, cfg), out_shape=jax.Shape...  18.9 us
    unnamed x1, local copies, waits for them, and re-layouts  1.3 us

profile of v1, /device:TPU:0, one launch (start us, length us, event | category | flops | bytes accessed | tf_op | source)
XLA Modules:
  0.0 20.2 jit_solution(5139794258737266306)
XLA Ops:
  0.0 18.9 %block_attention.1 = f32[4,4,128]{2,1,0:T(4,128)} custom-call(bf16[4,4,4096]{2,1,0:T(4,128)(2,1)} %q_hbm.1, bf16[128,4,4096]{2,1,0:T(4,128)(2,1)} %k_hbm.1, bf16[128,4,4096]{2,1,0:T(4,128)(2,1)} %v_hbm.1, bf16[4,4,4096]{2,1,0:T(4,128)(2,1)} %lk_hbm.1, bf16[4,4,4096]{2,1,0:T(4,128)(2,1)} %lv_hbm.1, s32[4,16,16]{2,1,0:T(8,128)} %sel_ref.1), custom_call_target="tpu_custom_call" | custom-call | tf_op jit(solution)/shard_map/block_attention/pallas_call | solution.py:160
  19.0 1.3 %copy.8 = f32[4,4,128]{2,1,0:T(4,128)} copy(f32[4,4,128]{2,1,0:T(4,128)} %block_attention.1) | data formatting | bytes 16384

commit v2 on v1

--- a/solution.py
+++ b/solution.py
@@ -10,33 +10,50 @@
 
 AXES = ("gx", "gy", "gz")
 LANES = 128
-GROUPS = 4
 NEG = float("-inf")
 
 
-def kernel(sizes, cfg, q_hbm, k_hbm, v_hbm, lk_hbm, lv_hbm, sel_ref, out_ref,
-           qbuf, kbuf, vbuf, send, recv, qsem, ksem, vsem, send_sem, recv_sem):
+def kernel(sizes, pair, cfg, q_hbm, k_hbm, v_hbm, lk_hbm, lv_hbm, sel_ref, out_ref,
+           qbuf, kbuf, vbuf, send, merged, recv, swap, qsem, ksem, vsem, pair_send, pair_recv, send_sem, recv_sem):
     positions, batch, local_blocks, heads, width, drafts, columns = cfg
     nx, ny, nz = sizes
     count = nx * ny * nz
+    half = count // 2
     me = (lax.axis_index("gx") * ny + lax.axis_index("gy")) * nz + lax.axis_index("gz")
+    stride = math.prod(sizes[pair + 1:])
+    side = lax.rem(lax.axis_index(AXES[pair]), 2)
+    my_slot = me // (2 * stride) * stride + lax.rem(me, stride)
     per_head = width // LANES
     tiles = heads * per_head
     sharers = LANES // columns
+    side_tiles = stride // sharers
+    group_tiles = 2 * side_tiles
+    groups = tiles // group_tiles
+    group_heads = group_tiles // per_head
+    side_heads = side_tiles // per_head
     rows = batch * drafts
     tokens = positions * batch
-    group_heads = heads // GROUPS
-    group_tiles = group_heads * per_head
     my_group = (me // sharers) // group_tiles
     scale = 1.0 / math.sqrt(width)
+    mesh_ids = pl.DeviceIdType.MESH
 
     def device_of(d):
         return {"gx": d // (ny * nz), "gy": (d // nz) % ny, "gz": d % nz}
 
     def group_at(step):
-        return lax.rem(my_group + 1 + step, GROUPS)
-
-    for step in range(GROUPS):
+        return lax.rem(my_group + 1 + step, groups)
+
+    barrier = pltpu.get_barrier_semaphore()
+    partner = {AXES[pair]: lax.axis_index(AXES[pair]) + 1 - 2 * side}
+    pl.semaphore_signal(barrier, inc=1, device_id=partner, device_id_type=mesh_ids)
+
+    def greet(i, _):
+        slot = lax.rem(my_slot + i, half)
+        d = slot // stride * (2 * stride) + side * stride + lax.rem(slot, stride)
+        pl.semaphore_signal(barrier, inc=1, device_id=device_of(d), device_id_type=mesh_ids)
+        return 0
+
+    for step in range(groups):
         g = group_at(step)
 
         def start(i, _, g=g, step=step):
@@ -50,25 +67,28 @@
             return 0
 
         lax.fori_loop(0, group_tiles, start, 0)
-
-    barrier = pltpu.get_barrier_semaphore()
-
-    def greet(i, _):
-        pl.semaphore_signal(barrier, inc=1, device_id=device_of(lax.rem(me + i, count)), device_id_type=pl.DeviceIdType.MESH)
-        return 0
-
-    lax.fori_loop(1, count, greet, 0)
+        if step == 0:
+            lax.fori_loop(1, half, greet, 0)
 
     total_rows = tokens + local_blocks * batch
     block_cols = tokens // local_blocks
     same = (lax.broadcasted_iota(jnp.int32, (rows, block_cols), 1) % batch
             == lax.broadcasted_iota(jnp.int32, (rows, block_cols), 0) // drafts)
-    same_lm = same[:, :local_blocks * batch]
-    lm_bias = jnp.where(same_lm, 0.0, NEG)
+    lm_bias = jnp.where(same[:, :local_blocks * batch], 0.0, NEG)
     lane = lax.broadcasted_iota(jnp.int32, (rows, LANES), 1)
     row = lax.broadcasted_iota(jnp.int32, (rows, LANES), 0)
 
-    def compute(step, _):
+    def stat_row(peak, total):
+        spread = jnp.where(lane == row, peak, jnp.where(lane == row + rows, total, 0.0))
+        return jnp.sum(spread, axis=0, keepdims=True)
+
+    def stat_columns(line):
+        line = jnp.broadcast_to(line, (rows, LANES))
+        peak = jnp.sum(jnp.where(lane == row, line, 0.0), axis=1, keepdims=True)
+        total = jnp.sum(jnp.where(lane == row + rows, line, 0.0), axis=1, keepdims=True)
+        return peak, total
+
+    def compute(step):
         g = group_at(step)
         span = pl.ds(g * group_tiles, group_tiles)
         pltpu.make_async_copy(qbuf.at[span], qbuf.at[span], qsem.at[step]).wait()
@@ -91,56 +111,85 @@
             w = jnp.exp(s - peak)
             total = jnp.sum(w, axis=1, keepdims=True)
             probs.append(w.astype(jnp.bfloat16))
-            spread = jnp.where(lane == row, peak, jnp.where(lane == row + rows, total, 0.0))
-            stats.append(jnp.sum(spread, axis=0, keepdims=True))
+            stats.append(stat_row(peak, total))
         pltpu.make_async_copy(vbuf.at[span], vbuf.at[span], vsem.at[step]).wait()
         for i in range(group_heads):
             h = g * group_heads + i
             v = jnp.concatenate([vbuf[h * per_head + c].reshape(total_rows, LANES) for c in range(per_head)], axis=1)
             o = jnp.dot(probs[i], v, preferred_element_type=jnp.float32)
             for c in range(per_head):
-                u = h * per_head + c
-                send[u, pl.ds(0, rows), :] = o[:, c * LANES:(c + 1) * LANES]
-                send[u, pl.ds(rows, 8), :] = jnp.broadcast_to(stats[i], (8, LANES))
-
-        @pl.when(step == 0)
-        def _():
-            pl.semaphore_wait(barrier, count - 1)
-
-        def post(i, _):
-            d = g * group_tiles * sharers + i
-            u = d // sharers
+                u = i * per_head + c
+                send[step, u, pl.ds(0, rows), :] = o[:, c * LANES:(c + 1) * LANES]
+                send[step, u, pl.ds(rows, 1), :] = stats[i]
+
+    def swap_copy(step):
+        return pltpu.make_async_remote_copy(
+            src_ref=send.at[step, pl.ds((1 - side) * side_tiles, side_tiles)], dst_ref=swap.at[step],
+            send_sem=pair_send.at[step], recv_sem=pair_recv.at[step],
+            device_id=partner, device_id_type=mesh_ids)
+
+    def merge(step):
+        swap_copy(step).wait_recv()
+        for i in range(side_heads):
+            first = side * side_tiles + i * per_head
+            peak0, total0 = stat_columns(send[step, first, pl.ds(rows, 1), :])
+            peak1, total1 = stat_columns(swap[step, i * per_head, pl.ds(rows, 1), :])
+            peak = jnp.maximum(peak0, peak1)
+            factor0 = jnp.exp(peak0 - peak)
+            factor1 = jnp.exp(peak1 - peak)
+            line = stat_row(peak, factor0 * total0 + factor1 * total1)
+            for c in range(per_head):
+                u = i * per_head + c
+                merged[step, u, pl.ds(0, rows), :] = (factor0 * send[step, first + c, pl.ds(0, rows), :]
+                                                      + factor1 * swap[step, u, pl.ds(0, rows), :])
+                merged[step, u, pl.ds(rows, 1), :] = line
+
+    def post(step):
+        base = (group_at(step) * group_tiles + side * side_tiles) * sharers
+
+        def one(i, _):
+            d = base + i
+            u = i // sharers
 
             @pl.when(d == me)
             def _():
-                pltpu.make_async_copy(send.at[u], recv.at[me], recv_sem).start()
+                recv[my_slot] = merged[step, u]
 
             @pl.when(d != me)
             def _():
                 pltpu.make_async_remote_copy(
-                    src_ref=send.at[u], dst_ref=recv.at[me], send_sem=send_sem, recv_sem=recv_sem,
-                    device_id=device_of(d), device_id_type=pl.DeviceIdType.MESH).start()
+                    src_ref=merged.at[step, u], dst_ref=recv.at[my_slot], send_sem=send_sem, recv_sem=recv_sem,
+                    device_id=device_of(d), device_id_type=mesh_ids).start()
             return 0
 
-        lax.fori_loop(0, group_tiles * sharers, post, 0)
-        return 0
-
-    lax.fori_loop(0, GROUPS, compute, 0)
-
-    pltpu.make_async_copy(recv, recv, recv_sem).wait()
-    gathered = recv[:, rows, :]
-    flipped = gathered.T
+        lax.fori_loop(0, side_tiles * sharers, one, 0)
+
+    for step in range(groups):
+        compute(step)
+        if step == 0:
+            pl.semaphore_wait(barrier, half)
+        swap_copy(step).start()
+        if step > 0:
+            merge(step - 1)
+            post(step - 1)
+    merge(groups - 1)
+    post(groups - 1)
+
+    others = pl.ds(0, half - 1)
+    for step in range(groups):
+        swap_copy(step).wait_send()
+    pltpu.make_async_copy(recv.at[others], recv.at[others], send_sem).wait()
+    pltpu.make_async_copy(recv.at[others], recv.at[others], recv_sem).wait()
+    flipped = recv[:, rows, :].T
     peaks = flipped[:rows]
     totals = flipped[rows:2 * rows]
     top = jnp.max(peaks, axis=1, keepdims=True)
     factor = jnp.exp(peaks - top)
     denominator = jnp.sum(factor * totals, axis=1, keepdims=True)
     numerator = jnp.zeros((rows, LANES), jnp.float32)
-    for s in range(count):
+    for s in range(half):
         numerator = numerator + factor[:, s:s + 1] * recv[s, pl.ds(0, rows), :]
     out_ref[...] = (numerator / denominator).reshape(batch, drafts, LANES)
-    others = pl.ds(0, count - 1)
-    pltpu.make_async_copy(recv.at[others], recv.at[others], send_sem).wait()
 
 
 def body(sizes, query, keys, values, lm_keys, lm_values, selected):
@@ -150,15 +199,20 @@
     width = feature // heads
     drafts = query.shape[1]
     count = math.prod(sizes)
-    columns = feature // count
+    columns = min(feature // count, LANES)
     tiles = feature // LANES
     rows = batch * drafts
     cfg = (positions, batch, local_blocks, heads, width, drafts, columns)
+    pair = sizes.index(max(sizes))
+    stride = math.prod(sizes[pair + 1:])
+    side_tiles = stride * columns // LANES
+    groups = tiles // (2 * side_tiles)
+    message = rows + 1
     anywhere = pl.BlockSpec(memory_space=pl.ANY)
     vmem = pl.BlockSpec(memory_space=pltpu.VMEM)
     span = positions + local_blocks
     out = pl.pallas_call(
-        functools.partial(kernel, sizes, cfg),
+        functools.partial(kernel, sizes, pair, cfg),
         out_shape=jax.ShapeDtypeStruct((batch, drafts, LANES), jnp.float32),
         in_specs=[anywhere] * 5 + [vmem],
         out_specs=vmem,
@@ -166,11 +220,15 @@
             pltpu.VMEM((tiles, batch, drafts, LANES), jnp.bfloat16),
             pltpu.VMEM((tiles, span, batch, LANES), jnp.bfloat16),
             pltpu.VMEM((tiles, span, batch, LANES), jnp.bfloat16),
-            pltpu.VMEM((tiles, rows + 8, LANES), jnp.float32),
-            pltpu.VMEM((count, rows + 8, LANES), jnp.float32),
-            pltpu.SemaphoreType.DMA((GROUPS,)),
-            pltpu.SemaphoreType.DMA((GROUPS,)),
-            pltpu.SemaphoreType.DMA((GROUPS,)),
+            pltpu.VMEM((groups, 2 * side_tiles, message, LANES), jnp.float32),
+            pltpu.VMEM((groups, side_tiles, message, LANES), jnp.float32),
+            pltpu.VMEM((count // 2, message, LANES), jnp.float32),
+            pltpu.VMEM((groups, side_tiles, message, LANES), jnp.float32),
+            pltpu.SemaphoreType.DMA((groups,)),
+            pltpu.SemaphoreType.DMA((groups,)),
+            pltpu.SemaphoreType.DMA((groups,)),
+            pltpu.SemaphoreType.DMA((groups,)),
+            pltpu.SemaphoreType.DMA((groups,)),
             pltpu.SemaphoreType.DMA,
             pltpu.SemaphoreType.DMA,
         ],

time: 20.5 us -> 17.2 us (0.84)
  Pallas kernels: 18.9 us -> 15.6 us
    pallas_call x1, Pallas kernels: 18.9 us -> 15.6 us  [body(): pl.pallas_call(functools.partial(kernel, sizes, pair, cfg), out_shape=jax...]
where the time goes in v2:
time: 17.2 us; the launch traced here: 17 us
  Pallas kernels  15.6 us (91%)
  local copies, waits for them, and re-layouts  1.3 us (8%)
    pallas_call x1, Pallas kernels, body(): pl.pallas_call(functools.partial(kernel, sizes, pair, cfg), out_shape=jax...  15.6 us
    unnamed x1, local copies, waits for them, and re-layouts  1.3 us

profile of v2, /device:TPU:0, one launch (start us, length us, event | category | flops | bytes accessed | tf_op | source)
XLA Modules:
  0.0 17.0 jit_solution(17878445631807669269)
XLA Ops:
  0.0 15.6 %block_attention.1 = f32[4,4,128]{2,1,0:T(4,128)} custom-call(bf16[4,4,4096]{2,1,0:T(4,128)(2,1)} %q_hbm.1, bf16[128,4,4096]{2,1,0:T(4,128)(2,1)} %k_hbm.1, bf16[128,4,4096]{2,1,0:T(4,128)(2,1)} %v_hbm.1, bf16[4,4,4096]{2,1,0:T(4,128)(2,1)} %lk_hbm.1, bf16[4,4,4096]{2,1,0:T(4,128)(2,1)} %lv_hbm.1, s32[4,16,16]{2,1,0:T(8,128)} %sel_ref.1), custom_call_target="tpu_custom_call" | custom-call | tf_op jit(solution)/shard_map/block_attention/pallas_call | solution.py:214
  15.7 1.3 %copy.8 = f32[4,4,128]{2,1,0:T(4,128)} copy(f32[4,4,128]{2,1,0:T(4,128)} %block_attention.1) | data formatting | bytes 16384
